TPU v7x, 32 devices: a whole 2x2x4 slice. The times are simulated.
32 devices in a mesh: row: 4 (over x, core), col: 8 (over z, y).
Axes of the slice: x: 2, y: 2, z: 4, core: 2. Of those that a mesh axis runs over, the one named last changes fastest.
Arguments:
- pooled: bfloat16 [2048, 1152], P(('row', 'col')), may hold values from -32 to 32
- hidden: bfloat16 [2048, 4304], P(('row', 'col')), may hold values from -6 to 6
- text: bfloat16 [2048, 1152], P(('row', 'col')), may hold values from -12 to 12
- weight: float32 [1152, 4304], P('col', 'row'), may hold values from -0.09375 to 0.09375
- row_moment: float32 [1152], P('col'), may hold values from 1e-07 to 1e-05
- col_moment: float32 [4304], P('row'), may hold values from 1e-07 to 1e-05
- log_scale: float32 [], replicated, may hold values from 4.2 to 4.8
- bias: float32 [], replicated, may hold values from -16 to -12
Outputs:
- update: float32 [1152, 4304], P('col', 'row')
- new_row: float32 [1152], P('col')
- new_col: float32 [4304], P('row')
- loss: float32 [], replicated
All inputs are finite; a program needn't handle non-finite values.
Results may differ from a plain program's by a relative error of at most 0.004.
Values may be sent and summed in bfloat16 or wider, within the bound.
A program may use at most 128 MiB of HBM per device.

v0:
```python
import jax
import jax.numpy as jnp
from jax import lax
from jax.sharding import PartitionSpec as P

D = 1152
FF = 4304


EPSILON = 1e-06
DECAY_RATE = 0.8
CLIP_LEVEL = 1.0
FLOOR_VALUE = 1e-30


def over_row_index(positions, column, tokens, columns):
    return (positions // tokens * columns + column) * tokens + positions % tokens


def over_col_index(positions, row_place, tokens, columns):
    return row_place * columns * tokens + positions


def pair_tile(images, image_ids, texts, text_ids, logit_scale, bias, batch_total):
    logits = logit_scale * jnp.dot(images, texts.T, preferred_element_type=jnp.float32) + bias
    label_sign = jnp.where(
        image_ids[:, None] == text_ids[None, :], jnp.float32(1.0), jnp.float32(-1.0)
    )
    loss_sum = jnp.sum(jax.nn.softplus(-label_sign * logits))
    grad_logits = (-label_sign * jax.nn.sigmoid(-label_sign * logits) / batch_total).astype(
        jnp.bfloat16
    )
    return (loss_sum, logit_scale * jnp.dot(grad_logits, texts, preferred_element_type=jnp.float32))


def per_device(pooled, hidden, text, weight, row_moment, col_moment, log_scale, bias):
    rows_count = lax.axis_size("row")
    cols_count = lax.axis_size("col")
    row_place = lax.axis_index("row")
    col_place = lax.axis_index("col")
    tokens = pooled.shape[0]
    batch_total = tokens * rows_count * cols_count
    split_hidden = lax.all_to_all(hidden, "row", split_axis=1, concat_axis=0, tiled=True)
    hidden_cols = split_hidden.shape[1]
    weight_half = weight.astype(jnp.bfloat16)
    grouped = split_hidden.reshape(rows_count, tokens, hidden_cols)
    hidden_all = lax.all_gather(grouped, "col", axis=1, tiled=True).reshape(
        batch_total, hidden_cols
    )
    partial_proj = lax.dot_general(
        weight_half, hidden_all, (((1,), (1,)), ((), ())), preferred_element_type=jnp.float32
    )
    summed = lax.psum_scatter(partial_proj, "row", scatter_dimension=1, tiled=True)
    projected = lax.all_to_all(summed, "col", split_axis=1, concat_axis=0, tiled=True).T
    mixed_rows = pooled.astype(jnp.float32) + projected
    length = jnp.sqrt(jnp.sum(mixed_rows * mixed_rows, axis=1, keepdims=True) + EPSILON)
    image_unit = mixed_rows / length
    images = image_unit.astype(jnp.bfloat16)
    text_float = text.astype(jnp.float32)
    text_units = (
        text_float / jnp.sqrt(jnp.sum(text_float * text_float, axis=1, keepdims=True) + EPSILON)
    ).astype(jnp.bfloat16)
    logit_scale = jnp.exp(log_scale)
    image_rows = lax.all_gather(images, "row", axis=0, tiled=True)
    image_ids = over_row_index(
        jnp.arange(image_rows.shape[0], dtype=jnp.int32), col_place, tokens, cols_count
    )
    piece = lax.all_gather(text_units, "col", axis=0, tiled=True)
    text_ids = over_col_index(
        jnp.arange(piece.shape[0], dtype=jnp.int32), row_place, tokens, cols_count
    )
    loss_local, unit_part = pair_tile(
        image_rows, image_ids, piece, text_ids, logit_scale, bias, batch_total
    )
    unit_grad = lax.psum_scatter(unit_part, "row", scatter_dimension=0, tiled=True)
    mixed_grad = (
        (unit_grad - image_unit * jnp.sum(image_unit * unit_grad, axis=1, keepdims=True)) / length
    ).astype(jnp.bfloat16)
    grad_cols = lax.all_to_all(mixed_grad.T, "col", split_axis=0, concat_axis=1, tiled=True)
    gradient = jnp.dot(
        lax.all_gather(grad_cols, "row", axis=1, tiled=True),
        hidden_all,
        preferred_element_type=jnp.float32,
    )
    squared = gradient * gradient + FLOOR_VALUE
    row_sum = lax.psum(jnp.sum(squared, axis=1), "row")
    col_sum = lax.psum(jnp.sum(squared, axis=0), "col")
    new_row = DECAY_RATE * row_moment + (1.0 - DECAY_RATE) * row_sum / FF
    new_col = DECAY_RATE * col_moment + (1.0 - DECAY_RATE) * col_sum / D
    second = new_row[:, None] * new_col[None, :]
    raw_update = gradient / jnp.sqrt(second)
    loss_total = lax.psum(loss_local, ("row", "col"))
    update_total = lax.psum(jnp.sum(raw_update * raw_update), ("row", "col"))
    update_rms = jnp.sqrt(update_total / (D * FF))
    update = raw_update / jnp.maximum(1.0, update_rms / CLIP_LEVEL)
    loss = loss_total / batch_total
    return (update, new_row, new_col, loss)


def solution(mesh):
    return jax.shard_map(
        per_device,
        mesh=mesh,
        in_specs=(
            P(("row", "col"), None),
            P(("row", "col"), None),
            P(("row", "col"), None),
            P("col", "row"),
            P("col"),
            P("row"),
            P(),
            P(),
        ),
        out_specs=(P("col", "row"), P("col"), P("row"), P()),
        check_vma=False,
    )
```

profile of v0, /device:TPU:0, one launch (start us, length us, event | category | flops | bytes accessed | tf_op | source)
XLA Modules:
  0.0 324.0 jit_solution(10579943734243616240)
XLA Ops:
  7.2 0.0 all-gather.3.cloned.1.call-start
  7.2 1.5 all_to_all.40
  8.7 0.1 copy.22
  8.8 13.6 %all_to_all.54 = bf16[64,4,1076]{2,0,1:T(8,128)(2,1)S(1)} all-to-all(bf16[64,4,1076]{2,0,1:T(8,128)(2,1)S(1)} %copy.22), channel_id=1, replica_groups=mesh['row'=4,'col'=8] {'row'}, dimensions={1} | all-to-all | bytes 1101824 | tf_op jit(solution)/shard_map/all_to_all | solution.py:43
  22.3 1.3 copy.23
  23.6 0.0 all-gather.3.cloned.1.call-update
  23.6 0.0 reduce-scatter.3.cloned.1.call-start
  23.7 79.8 %all-gather.3.cloned.1.call-done = bf16[4,512,1076]{2,0,1:T(4,128)(2,1)} async-done(((bf16[4,64,1076]{2,0,1:T(4,128)(2,1)}), bf16[4,512,1076]{2,0,1:T(4,128)(2,1)}) %all-gather.3.cloned.1.call-update) | async-done | bytes 4407312 | tf_op jit(solution)/shard_map/all_gather | solution.py:47
  103.4 10.4 %copy.24 = bf16[4,512,1076]{1,0,2:T(4,128)(2,1)} copy(bf16[4,512,1076]{2,0,1:T(4,128)(2,1)} %all-gather.3.cloned.1.call-done) | data formatting | bytes 8814592 | tf_op jit(solution)/shard_map/all_gather | solution.py:47
  113.8 3.9 %pad = bf16[1080,4,512]{2,1,0:T(4,128)(2,1)S(1)} pad(bf16[1076,4,512]{2,1,0:T(4,128)(2,1)} %bitcast.38, bf16[]{:T(256)} %constant.79), padding=0_4x0_0x0_0 | pad | bytes 8830978
  117.7 1.9 copy.31
  119.6 2.0 copy-done
  121.6 2.2 fusion.6
  123.9 0.0 reduce-scatter.3.cloned.1.call-update
  123.9 0.0 all-gather.5.cloned.1.call-start
  123.9 0.8 copy-done.3
  124.8 0.1 fusion.8
  124.9 0.8 fusion.9
  125.7 0.0 all-gather.5.cloned.1.call-update
  125.7 22.3 %reduce-scatter.3.cloned.1.call-done = f32[144,512]{1,0:T(8,128)} async-done(((f32[144,2048]{1,0:T(8,128)}), f32[144,512]{1,0:T(8,128)}) %reduce-scatter.3.cloned.1.call-update) | async-done | bytes 294928 | tf_op jit(solution)/shard_map/reduce_scatter | solution.py:53
  148.0 2.0 copy.29
  150.0 5.5 %all-to-all-start.1 = ((f32[144,8,64]{0,2,1:T(8,128)}), f32[144,8,64]{0,2,1:T(8,128)S(1)}, u32[]{:S(2)}, u32[]{:S(2)}) async-start(f32[144,8,64]{0,2,1:T(8,128)} %bitcast.1), calls=%async_computation.2 | async-start | bytes 1048576 | tf_op jit(solution)/shard_map/all_to_all | solution.py:54
  155.5 0.0 reduce-scatter.5.cloned.1.call-start
  156.9 17.6 %all-to-all-done.1 = f32[144,8,64]{0,2,1:T(8,128)S(1)} async-done(((f32[144,8,64]{0,2,1:T(8,128)}), f32[144,8,64]{0,2,1:T(8,128)S(1)}, u32[]{:S(2)}, u32[]{:S(2)}) %all-to-all-start.1) | async-done | bytes 294944 | tf_op jit(solution)/shard_map/all_to_all | solution.py:54
  174.5 0.3 copy.26
  174.8 0.2 all_to_all.46
  175.1 0.1 multiply_reduce_fusion.2
  175.2 0.1 fusion.26
  175.3 6.7 %all_gather.13 = bf16[256,1152]{1,0:T(8,128)(2,1)S(1)} all-gather(bf16[64,1152]{1,0:T(8,128)(2,1)S(1)} %fusion.26), channel_id=1, replica_groups=mesh['row'=4,'col'=8] {'row'}, dimensions={0}, use_global_device_ids=true | all-gather | bytes 737280 | tf_op jit(solution)/shard_map/all_gather | solution.py:64
  182.0 11.8 %all-gather.5.cloned.1.call-done = bf16[512,1152]{1,0:T(8,128)(2,1)} async-done(((bf16[64,1152]{1,0:T(8,128)(2,1)}), bf16[512,1152]{1,0:T(8,128)(2,1)}) %all-gather.5.cloned.1.call-update) | async-done | bytes 1179664 | tf_op jit(solution)/shard_map/all_gather | solution.py:68
  193.9 2.9 fusion.5
  196.7 1.6 convolution_multiply_fusion
  198.4 0.0 reduce-scatter.5.cloned.1.call-update
  198.4 24.4 %reduce-scatter.5.cloned.1.call-done = f32[64,1152]{1,0:T(8,128)} async-done(((f32[256,1152]{1,0:T(8,128)}), f32[64,1152]{1,0:T(8,128)}) %reduce-scatter.5.cloned.1.call-update) | async-done | bytes 294928 | tf_op jit(solution)/shard_map/reduce_scatter | solution.py:75
  222.8 1.2 multiply_reduce_fusion.1
  224.0 1.1 fusion.16
  225.1 0.4 all_to_all.47
  225.5 14.1 %all_to_all.55 = bf16[8,144,64]{1,2,0:T(8,128)(2,1)S(1)} all-to-all(bf16[8,144,64]{1,2,0:T(8,128)(2,1)S(1)} %copy.27), channel_id=1, replica_groups=mesh['row'=4,'col'=8] {'col'}, dimensions={0} | all-to-all | bytes 294912 | tf_op jit(solution)/shard_map/all_to_all | solution.py:79
  239.6 0.1 copy.30
  239.7 6.7 %all_gather.15 = bf16[144,2048]{1,0:T(8,128)(2,1)S(1)} all-gather(bf16[144,512]{1,0:T(8,128)(2,1)S(1)} %copy.30), channel_id=1, replica_groups=mesh['row'=4,'col'=8] {'row'}, dimensions={1}, use_global_device_ids=true | all-gather | bytes 737280 | tf_op jit(solution)/shard_map/all_gather | solution.py:81
  246.4 4.1 %fusion.3 = (f32[144]{0:T(256)S(1)}, f32[1076]{0:T(1024)S(1)}, f32[144,1076]{1,0:T(8,128)S(1)}) fusion(bf16[144,2048]{1,0:T(8,128)(2,1)S(1)} %all_gather.15, bf16[2048,1076]{0,1:T(8,128)(2,1)} %bitcast.36), kind=kOutput, calls=%fused_computation.9 | convolution fusion | flops 635269184 | bytes 5621776 | tf_op jit(solution)/shard_map/dot_general | solution.py:80
  250.4 19.8 %psum.29 = f32[1076]{0:T(1024)S(1)} all-reduce(f32[1076]{0:T(1024)S(1)} %get-tuple-element.5), channel_id=1, replica_groups=mesh['row'=4,'col'=8] {'col'}, use_global_device_ids=true, to_apply=%region_8.9 | all-reduce | flops 1076 | bytes 8608 | tf_op jit(solution)/shard_map/psum | solution.py:87
  270.2 5.7 %psum.28 = f32[144]{0:T(256)S(1)} all-reduce(f32[144]{0:T(256)S(1)} %get-tuple-element.4), channel_id=1, replica_groups=mesh['row'=4,'col'=8] {'row'}, use_global_device_ids=true, to_apply=%region_6.7 | all-reduce | flops 144 | bytes 1152 | tf_op jit(solution)/shard_map/psum | solution.py:86
  275.9 0.0 copy-start.4
  275.9 0.0 copy-start.5
  275.9 0.9 multiply_reduce_fusion
  276.9 37.1 %all-reduce = (f32[]{:T(128)}, f32[]{:T(128)}) all-reduce(f32[]{:T(128)} %multiply_reduce_fusion, f32[]{:T(128)} %get-tuple-element.9), channel_id=1, replica_groups=mesh['row'=4,'col'=8] {'row','col'}, use_global_device_ids=true, to_apply=%region_10.11 | all-reduce | flops 2 | bytes 16 | tf_op jit(solution)/shard_map/psum | solution.py:93
  314.6 1.0 fusion.4
  (21 shorter events, 0.1 us)
Async XLA Ops:
  7.2 96.3 %all-gather.3.cloned.1.call-start = ((), (), s32[]{:S(2)}) async-start(), calls=%async_computation.5 | async-start | bytes 5308416 | tf_op jit(solution)/shard_map/all_gather | solution.py:47
  23.6 124.4 %reduce-scatter.3.cloned.1.call-start = ((), (), s32[]{:S(2)}) async-start(), calls=%async_computation.6 | async-start | bytes 1474560 | tf_op jit(solution)/shard_map/reduce_scatter | solution.py:53
  117.7 3.9 %copy-start.2 = (f32[144,1076]{1,0:T(8,128)S(1)}, f32[144,1076]{1,0:T(8,128)}, u32[]{:S(2)}) copy-start(f32[144,1076]{1,0:T(8,128)} %param.11) | copy-start | bytes 1859332
  119.6 2.0 copy-start
  123.9 0.9 copy-start.3
  123.9 70.0 %all-gather.5.cloned.1.call-start = ((), (), s32[]{:S(2)}) async-start(), calls=%async_computation.7 | async-start | bytes 1327104 | tf_op jit(solution)/shard_map/all_gather | solution.py:68
  150.0 24.6 %all-to-all-start.1 = ((f32[144,8,64]{0,2,1:T(8,128)}), f32[144,8,64]{0,2,1:T(8,128)S(1)}, u32[]{:S(2)}, u32[]{:S(2)}) async-start(f32[144,8,64]{0,2,1:T(8,128)} %bitcast.1), calls=%async_computation.2 | async-start | bytes 1048576 | tf_op jit(solution)/shard_map/all_to_all | solution.py:54
  155.5 19.6 %copy-start.1 = (bf16[64,1152]{1,0:T(8,128)(2,1)S(1)}, bf16[64,1152]{1,0:T(8,128)(2,1)}, u32[]{:S(2)}) copy-start(bf16[64,1152]{1,0:T(8,128)(2,1)} %param.8) | copy-start | bytes 442372
  155.5 67.3 %reduce-scatter.5.cloned.1.call-start = ((), (), s32[]{:S(2)}) async-start(), calls=%async_computation.8 | async-start | bytes 1474560 | tf_op jit(solution)/shard_map/reduce_scatter | solution.py:75
  193.8 2.9 copy-start.8
  246.4 29.5 %copy-start.6 = (f32[1076]{0:T(1024)S(1)}, f32[1076]{0:T(1024)}, u32[]{:S(2)}) copy-start(f32[1076]{0:T(1024)} %param.13) | copy-start | bytes 12916
  246.4 29.5 %copy-start.7 = (f32[144]{0:T(256)S(1)}, f32[144]{0:T(256)}, u32[]{:S(2)}) copy-start(f32[144]{0:T(256)} %param.12) | copy-start | bytes 1732
  275.9 40.4 %copy-start.4 = (f32[1076]{0:T(1024)}, f32[1076]{0:T(1024)S(1)}, u32[]{:S(2)}) copy-start(f32[1076]{0:T(1024)S(1)} %multiply_add_fusion.1) | copy-start | bytes 12916
  275.9 40.4 %copy-start.5 = (f32[144]{0:T(256)}, f32[144]{0:T(256)S(1)}, u32[]{:S(2)}) copy-start(f32[144]{0:T(256)S(1)} %multiply_add_fusion.2) | copy-start | bytes 1732
Sparse Core Ops, SparseCore 0:
  23.8 79.6 all-gather.2
  124.0 23.9 reduce-scatter.2
  150.2 43.5 all-gather.4
  198.5 24.2 reduce-scatter.4
where the time goes:
time: 326 us; the launch traced here: 324 us
  waiting for transfers between devices  156 us (48%)
  blocking collectives  104 us (32%)
  local copies, waits for them, and re-layouts  24.9 us (8%)
  between operations  17.8 us (5%)
  matrix products  10.8 us (3%)
  starting transfers between devices  5.67 us (2%)
  other arithmetic  5.36 us (2%)
    all_gather x1, waiting for transfers between devices, per_device(): lax.all_gather(grouped, 'col', axis=1, tiled=True)  79.8 us
    psum x1, blocking collectives, per_device(): update_total = lax.psum(jnp.sum(raw_update * raw_update), ('row', 'col'))  37.1 us
    reduce_scatter x1, waiting for transfers between devices, per_device(): lax.psum_scatter(unit_part, 'row', scatter_dimension=0, tiled=True)  24.4 us
    reduce_scatter x1, waiting for transfers between devices, per_device(): lax.psum_scatter(partial_proj, 'row', scatter_dimension=1, tiled=True)  22.3 us
    psum x1, blocking collectives, per_device(): col_sum = lax.psum(jnp.sum(squared, axis=0), 'col')  19.8 us
    all_to_all x1, waiting for transfers between devices, per_device(): lax.all_to_all(summed, 'col', split_axis=1, concat_axis=0, tiled=True)  17.6 us
    all_to_all x1, blocking collectives, per_device(): lax.all_to_all(mixed_grad.T, 'col', split_axis=0, concat_axis=1, tiled=True)  14.1 us
    all_to_all x1, blocking collectives, per_device(): lax.all_to_all(hidden, 'row', split_axis=1, concat_axis=0, tiled=True)  13.6 us
  transfers between devices with their start and end apart: 5, of which 5 were waited for; matrix products, arithmetic and copies ran while one was open for 1% of the time, Pallas kernels for 0%

commit v1 on v0

v1 whole, which is shorter than its diff:
```python
import functools

import jax
import jax.numpy as jnp
from jax import lax
from jax.experimental import pallas as pl
from jax.experimental.pallas import tpu as pltpu
from jax.sharding import PartitionSpec as P

EPSILON = 1e-06
DECAY_RATE = 0.8
CLIP_LEVEL = 1.0
FLOOR_VALUE = 1e-30
CORES = 2
LOW = 2
MESH = pl.DeviceIdType.MESH
F32 = jnp.float32
BF16 = jnp.bfloat16


def dot_nt(a, b):
    return lax.dot_general(a, b, (((1,), (1,)), ((), ())), preferred_element_type=F32)


def kernel(
    sizes,
    hs_ref, wh_ref, pool_ref, tx_ref, rm_ref, cm_ref, ls_ref, bias_ref,
    upd_ref, nr_ref, nc_ref, loss_ref,
    hid, wg, txa, part, proj, img_s, img_r, ug_s, ug_r, mg_s, mga, gz_s, gz,
    rsb, csb, stb,
    hid_ss, hid_rs, w_ss, w_rs, tz_ss, tp_ss, t_rs, p_ss, p_rs, pair_ss, pair_rs,
    mg_ss, mg_rs, g_ss, g_rs, row_ss, row_rs, col_ss, col_rs, st_ss, st_rs,
):
    R, C, X, Z, T, Db, Dp, Fb, chunk = sizes
    L = LOW
    plane = R * L
    devices = R * C
    batch = devices * T
    r = lax.axis_index("row")
    c = lax.axis_index("col")
    z, y = c // L, c % L
    x, core = r // CORES, r % CORES
    q = r * L + y
    finish = []

    def send(src, dst, ss, rs, device, cond=None):
        def make():
            return pltpu.make_async_remote_copy(
                src_ref=src, dst_ref=dst, send_sem=ss, recv_sem=rs,
                device_id=device, device_id_type=MESH,
            )

        if cond is None:
            make().start()
            finish.append(lambda: make().wait_send())
        else:
            pl.when(cond)(lambda: make().start())
            finish.append(lambda: pl.when(cond)(lambda: make().wait_send()))

    def arrived(slot, rs):
        pltpu.make_async_copy(slot, slot, rs).wait()

    def plane_peer(o):
        other = lax.rem(q + o, plane)
        return other, other // L, other % L

    def rows(index, count):
        return pl.ds(pl.multiple_of(index * count, count), count)

    for o in range(1, plane):
        _, r2, y2 = plane_peer(o)
        send(hs_ref.at[r2], hid.at[rows(q, T)], hid_ss.at[o], hid_rs.at[q], (r2, z * L + y2))
    hid[rows(q, T)] = hs_ref[r]

    wg[rows(z, Dp)] = wh_ref[...]
    own_slot = x * C + c
    txa[:, rows(own_slot, T), :] = tx_ref[...]

    def text_place(zs):
        return x * C + zs * L + y

    for s in range(Z):
        for d, direction in enumerate((1, -1)):
            zs = z - direction * s
            nz = z + direction
            has = jnp.logical_and(zs >= 0, zs < Z)
            go = jnp.logical_and(has, jnp.logical_and(nz >= 0, nz < Z))
            place = text_place(jnp.clip(zs, 0, Z - 1))
            at = txa.at[:, rows(place, T), :]
            source = tx_ref if s == 0 else at
            if s:
                pl.when(has)(lambda: arrived(at, t_rs.at[place]))
            send(source, at, tz_ss.at[d, s], t_rs.at[place], (r, jnp.clip(nz, 0, Z - 1) * L + y), go)
            if s or d == 0:
                mine = x * L + y
                for o in range(1, X * L):
                    other = lax.rem(mine + o, X * L)
                    send(
                        source, at, tp_ss.at[d, s, o], t_rs.at[place],
                        ((other // L) * CORES + core, z * L + other % L),
                        has if s else None,
                    )
        for d, direction in enumerate((1, -1)):
            zs = z - direction * s
            nz = z + direction
            has = jnp.logical_and(zs >= 0, zs < Z)
            go = jnp.logical_and(has, jnp.logical_and(nz >= 0, nz < Z))
            block = jnp.clip(zs, 0, Z - 1)
            at = wg.at[rows(block, Dp)]
            if s:
                pl.when(has)(lambda: arrived(at, w_rs.at[block]))
            send(
                wh_ref if s == 0 else at, at, w_ss.at[d, s], w_rs.at[block],
                (r, jnp.clip(nz, 0, Z - 1) * L + y), go,
            )
    for o in range(1, plane):
        other, _, _ = plane_peer(o)
        arrived(hid.at[rows(other, T)], hid_rs.at[other])

    part[...] = dot_nt(hid[...], wg[...])
    for o in range(1, plane):
        other, r2, y2 = plane_peer(o)
        send(part.at[rows(other, T)], proj.at[r, y], p_ss.at[o], p_rs.at[q], (r2, z * L + y2))
    proj[r, y] = part[rows(q, T)]
    for o in range(1, plane):
        other, r2, y2 = plane_peer(o)
        arrived(proj.at[r2, y2], p_rs.at[other])
    mixed = []
    for h in range(L):
        total = proj[0, h]
        for k in range(1, R):
            total = total + proj[k, h]
        mixed.append(pool_ref[h].astype(F32) + total)
    square = sum(jnp.sum(m * m, axis=1, keepdims=True) for m in mixed)
    length = jnp.sqrt(square + EPSILON)
    unit = [m / length for m in mixed]
    for h in range(L):
        img_s[h] = unit[h].astype(BF16)
    partner = (x * CORES + (1 - core), c)
    send(img_s, img_r, pair_ss.at[0], pair_rs.at[0], partner)

    for o in range(1, X * L):
        other = lax.rem(x * L + y + o, X * L)
        for zs in range(Z):
            place = (other // L) * C + zs * L + other % L
            arrived(txa.at[:, rows(place, T), :], t_rs.at[place])

    scale = jnp.exp(jnp.full((1, 1), ls_ref[0], F32))
    bias = jnp.full((1, 1), bias_ref[0], F32)
    steps = X * C * T // chunk

    def pairs(images, own):
        halves = [images[h] for h in range(L)]

        def step(i, carry):
            loss, grads = carry
            cut = pl.ds(pl.multiple_of(i * chunk, chunk), chunk)
            texts = [txa[h, cut, :] for h in range(L)]
            logits = scale * sum(dot_nt(halves[h], texts[h]) for h in range(L)) + bias
            if own:
                row_id = lax.broadcasted_iota(jnp.int32, logits.shape, 0) + own_slot * T
                col_id = lax.broadcasted_iota(jnp.int32, logits.shape, 1) + i * chunk
                sign = jnp.where(row_id == col_id, F32(1.0), F32(-1.0))
            else:
                sign = F32(-1.0)
            u = -sign * logits
            e = jnp.exp(-jnp.abs(u))
            loss = loss + jnp.sum(jnp.maximum(u, 0.0) + jnp.log1p(e), axis=1, keepdims=True)
            sig = jnp.where(u >= 0, F32(1.0), e) / (1.0 + e)
            pg = (-sign * sig / batch).astype(BF16)
            grads = tuple(
                grads[h] + jnp.dot(pg, texts[h], preferred_element_type=F32) for h in range(L)
            )
            return loss, grads

        zero = (jnp.zeros((T, 1), F32), tuple(jnp.zeros((T, Z * Dp), F32) for _ in range(L)))
        if steps == 1:
            return step(0, zero)
        return lax.fori_loop(0, steps, step, zero)

    arrived(img_r, pair_rs.at[0])
    loss_b, grads_b = pairs(img_r, False)
    for h in range(L):
        ug_s[h] = scale * grads_b[h]
    send(ug_s, ug_r, pair_ss.at[1], pair_rs.at[1], partner)
    loss_a, grads_a = pairs(img_s, True)
    arrived(ug_r, pair_rs.at[1])
    ug = [scale * grads_a[h] + ug_r[h] for h in range(L)]
    inner = sum(jnp.sum(unit[h] * ug[h], axis=1, keepdims=True) for h in range(L))
    for h in range(L):
        mg_s[h] = ((ug[h] - unit[h] * inner) / length).astype(BF16)
    for o in range(1, plane):
        _, r2, y2 = plane_peer(o)
        send(mg_s.at[y2], mga.at[rows(q, T)], mg_ss.at[o], mg_rs.at[q], (r2, z * L + y2))
    mga[rows(q, T)] = mg_s[y]
    for o in range(1, plane):
        other, _, _ = plane_peer(o)
        arrived(mga.at[rows(other, T)], mg_rs.at[other])

    turned = mga[...].T
    for zs in range(Z):
        gz_s[zs] = jnp.dot(
            turned[zs * Dp:(zs + 1) * Dp], hid[...], preferred_element_type=F32
        ).astype(BF16)
    for o in range(1, Z):
        z2 = lax.rem(z + o, Z)
        send(gz_s.at[z2], gz.at[z], g_ss.at[o], g_rs.at[z], (r, z2 * L + y))
    upd_ref[...] = own_block(turned, hid, z, Z, Dp, Db)
    for o in range(1, Z):
        z2 = lax.rem(z + o, Z)
        arrived(gz.at[z2], g_rs.at[z2])
        upd_ref[...] += gz[z2][:Db].astype(F32)
    g = upd_ref[...]

    sq = g * g + FLOOR_VALUE
    rsb[r] = jnp.sum(sq, axis=1, keepdims=True)
    csb[c] = jnp.sum(sq, axis=0, keepdims=True)
    for o in range(1, C):
        c2 = lax.rem(c + o, C)
        send(csb.at[c], csb.at[c], col_ss.at[o], col_rs.at[c], (r, c2))
    for o in range(1, R):
        r2 = lax.rem(r + o, R)
        send(rsb.at[r], rsb.at[r], row_ss.at[o], row_rs.at[r], (r2, c))
    for o in range(1, R):
        r2 = lax.rem(r + o, R)
        arrived(rsb.at[r2], row_rs.at[r2])
    for o in range(1, C):
        c2 = lax.rem(c + o, C)
        arrived(csb.at[c2], col_rs.at[c2])
    row_sum = sum(rsb[k] for k in range(R))
    col_sum = sum(csb[k] for k in range(C))
    new_row = DECAY_RATE * rm_ref[...] + (1.0 - DECAY_RATE) * row_sum / (R * Fb)
    new_col = DECAY_RATE * cm_ref[...] + (1.0 - DECAY_RATE) * col_sum / (C * Db)
    nr_ref[...] = new_row
    nc_ref[...] = new_col
    raw = g / jnp.sqrt(new_row * new_col)
    upd_ref[...] = raw
    local = jnp.sum(jnp.sum(raw * raw, axis=1, keepdims=True), axis=0, keepdims=True)
    loss_local = jnp.sum(loss_a + loss_b, axis=0, keepdims=True)
    lane = lax.broadcasted_iota(jnp.int32, (1, 128), 1)
    me = r * C + c
    stb[me] = jnp.where(lane == 0, local, loss_local)

    def tell(o, wait):
        other = lax.rem(me + o, devices)
        copy = pltpu.make_async_remote_copy(
            src_ref=stb.at[me], dst_ref=stb.at[me], send_sem=st_ss.at[o], recv_sem=st_rs.at[me],
            device_id=(other // C, other % C), device_id_type=MESH,
        )
        if wait:
            copy.wait_send()
            arrived(stb.at[other], st_rs.at[other])
        else:
            copy.start()

    def tell_start(o, _):
        tell(o, False)
        return _

    def tell_wait(o, _):
        tell(o, True)
        return _

    lax.fori_loop(1, devices, tell_start, 0)
    lax.fori_loop(1, devices, tell_wait, 0)
    totals = jnp.sum(stb[...], axis=0)
    rms = jnp.sqrt(totals[:, 0:1] / (C * Db * R * Fb))
    upd_ref[...] = upd_ref[...] / jnp.maximum(1.0, rms / CLIP_LEVEL)
    loss_ref[...] = totals / batch
    for wait in finish:
        wait()


def own_block(turned, hid, z, Z, Dp, Db):
    picked = turned[0:Dp]
    for zs in range(1, Z):
        picked = jnp.where(z == zs, turned[zs * Dp:(zs + 1) * Dp], picked)
    return jnp.dot(picked, hid[...], preferred_element_type=F32)[:Db]


def per_device(pooled, hidden, text, weight, row_moment, col_moment, log_scale, bias):
    R, C = lax.axis_size("row"), lax.axis_size("col")
    L, X, Z = LOW, R // CORES, C // LOW
    T, D = pooled.shape
    Db, Fb = weight.shape
    Dp = -(-Db // 16) * 16
    F2 = Z * Dp
    plane = R * L
    texts = X * C * T
    chunk = min(texts, 512)

    def by_half(a):
        a = a.reshape(T, Z, L, Db).transpose(2, 0, 1, 3)
        if Dp != Db:
            a = jnp.pad(a, ((0, 0), (0, 0), (0, 0), (0, Dp - Db)))
        return a.reshape(L, T, F2)

    hs = hidden.reshape(T, R, Fb).transpose(1, 0, 2)
    wh = weight.astype(BF16)
    if Dp != Db:
        wh = jnp.pad(wh, ((0, Dp - Db), (0, 0)))
    tf = text.astype(F32)
    tn = (tf / jnp.sqrt(jnp.sum(tf * tf, axis=1, keepdims=True) + EPSILON)).astype(BF16)
    sizes = (R, C, X, Z, T, Db, Dp, Fb, chunk)
    vmem = pl.BlockSpec(memory_space=pltpu.VMEM)
    smem = pl.BlockSpec(memory_space=pltpu.SMEM)
    dma = lambda *s: pltpu.SemaphoreType.DMA(s)
    upd, nr, nc, loss = pl.pallas_call(
        functools.partial(kernel, sizes),
        out_shape=(
            jax.ShapeDtypeStruct((Db, Fb), F32),
            jax.ShapeDtypeStruct((Db, 1), F32),
            jax.ShapeDtypeStruct((1, Fb), F32),
            jax.ShapeDtypeStruct((1, 128), F32),
        ),
        in_specs=[vmem] * 6 + [smem] * 2,
        out_specs=(vmem,) * 4,
        scratch_shapes=[
            pltpu.VMEM((plane * T, Fb), BF16),
            pltpu.VMEM((F2, Fb), BF16),
            pltpu.VMEM((L, texts, F2), BF16),
            pltpu.VMEM((plane * T, F2), F32),
            pltpu.VMEM((R, L, T, F2), F32),
            pltpu.VMEM((L, T, F2), BF16),
            pltpu.VMEM((L, T, F2), BF16),
            pltpu.VMEM((L, T, F2), F32),
            pltpu.VMEM((L, T, F2), F32),
            pltpu.VMEM((L, T, F2), BF16),
            pltpu.VMEM((plane * T, F2), BF16),
            pltpu.VMEM((Z, Dp, Fb), BF16),
            pltpu.VMEM((Z, Dp, Fb), BF16),
            pltpu.VMEM((R, Db, 1), F32),
            pltpu.VMEM((C, 1, Fb), F32),
            pltpu.VMEM((R * C, 1, 128), F32),
            dma(plane), dma(plane), dma(2, Z), dma(Z), dma(2, Z), dma(2, Z, X * L), dma(X * C),
            dma(plane), dma(plane), dma(2), dma(2), dma(plane), dma(plane), dma(Z), dma(Z),
            dma(R), dma(R), dma(C), dma(C), dma(R * C), dma(R * C),
        ],
        compiler_params=pltpu.CompilerParams(
            has_side_effects=True, vmem_limit_bytes=60 * 1024 * 1024
        ),
    )(
        hs, wh, by_half(pooled), by_half(tn), row_moment[:, None], col_moment[None, :],
        log_scale[None], bias[None],
    )
    return upd, nr[:, 0], nc[0], loss[0, 1]


def solution(mesh):
    return jax.shard_map(
        per_device,
        mesh=mesh,
        in_specs=(
            P(("row", "col"), None),
            P(("row", "col"), None),
            P(("row", "col"), None),
            P("col", "row"),
            P("col"),
            P("row"),
            P(),
            P(),
        ),
        out_specs=(P("col", "row"), P("col"), P("row"), P()),
        check_vma=False,
    )
```

time: 326 us -> 140 us (0.43)
  waiting for transfers between devices: 156 us -> 0 us
  Pallas kernels: 0 us -> 125 us
  blocking collectives: 104 us -> 0 us
  local copies, waits for them, and re-layouts: 24.9 us -> 9 us
  between operations: 17.8 us -> 2.08 us
  matrix products: 10.8 us -> 0 us
  starting transfers between devices: 5.67 us -> 0 us
    pallas_call x0 -> x1, Pallas kernels: none -> 125 us  [per_device(): pl.pallas_call(functools.partial(kernel, sizes), out_shape=(jax.ShapeDtyp...]
    all_gather x2 -> x0, waiting for transfers between devices: 91.6 us -> none  [the longest x1 79.8 us: per_device(): lax.all_gather(grouped, 'col', axis=1, tiled=True)]
    psum x3 -> x0, blocking collectives: 62.5 us -> none  [the longest x1 37.1 us: per_device(): update_total = lax.psum(jnp.sum(raw_update * raw_update), ('row', 'col'))]
    reduce_scatter x2 -> x0, waiting for transfers between devices: 46.7 us -> none  [the longest x1 24.4 us: per_device(): lax.psum_scatter(unit_part, 'row', scatter_dimension=0, tiled=True)]
    all_to_all x2 -> x0, blocking collectives: 27.6 us -> none  [the longest x1 14.1 us: per_device(): lax.all_to_all(mixed_grad.T, 'col', split_axis=0, concat_axis=1, tiled=True)]
    all_to_all x1 -> x0, waiting for transfers between devices: 17.6 us -> none  [per_device(): lax.all_to_all(summed, 'col', split_axis=1, concat_axis=0, tiled=True)]
    all_gather x2 -> x0, blocking collectives: 13.4 us -> none  [the longest x1 6.68 us: per_device(): lax.all_gather(grad_cols, 'row', axis=1, tiled=True)]
    dot_general x4 -> x0, matrix products: 10.8 us -> none  [the longest x1 4.06 us: per_device(): jnp.dot(lax.all_gather(grad_cols, 'row', axis=1, tiled=True), hidden_all,...]
  transfers between devices with their start and end apart: 5 -> 0, of which waited for: 5 -> 0; matrix products, arithmetic and copies ran while one was open for 1% -> 0% of each run, Pallas kernels for 0% -> 0%
where the time goes in v1:
time: 140 us
  Pallas kernels  125 us (89%)
  local copies, waits for them, and re-layouts  9 us (6%)
  other arithmetic  4.1 us (3%)
  between operations  2.08 us (1%)
    pallas_call x1, Pallas kernels, per_device(): pl.pallas_call(functools.partial(kernel, sizes), out_shape=(jax.ShapeDtyp...  125 us
    unnamed x17, local copies, waits for them, and re-layouts  3.11 us

profile of v1, /device:TPU:0, one launch (start us, length us, event | category | flops | bytes accessed | tf_op | source)
XLA Modules:
  0.0 139.9 jit_solution(13268459176406926110)
XLA Ops:
  0.6 0.0 copy-start.1
  2.0 0.0 copy-start.4
  2.0 1.0 fusion
  3.0 0.0 copy-done.4
  3.1 0.0 copy-start.6
  3.1 0.6 broadcast_in_dim.14.cm_ref
  3.7 0.1 copy-done.6
  3.7 0.7 copy.17.rm_ref
  4.5 0.0 copy-done.1
  4.5 0.1 fusion.1
  4.6 0.4 reshape.32
  5.0 0.1 copy.22
  5.1 0.0 copy-start.3
  5.1 0.9 reshape.33.tx_ref
  5.9 0.0 copy-done.3
  6.0 0.0 copy-start
  6.0 0.4 reshape.30
  6.3 0.1 copy.23
  6.5 0.9 reshape.31.pool_ref
  7.3 0.0 copy-done
  7.3 0.0 copy-start.2
  7.3 0.8 convert_element_type.9.wh_ref
  8.1 0.4 copy-done.2
  8.5 0.4 reshape.29
  8.9 0.9 copy.21
  9.8 124.7 %shard_map.111 = (f32[144,1076]{1,0:T(8,128)}, f32[144,1]{1,0:T(8,128)}, f32[1,1076]{1,0:T(1,128)}, f32[1,128]{1,0:T(1,128)}) custom-call(bf16[4,64,1076]{2,1,0:T(8,128)(2,1)} %bitcast.15, bf16[144,1076]{1,0:T(8,128)(2,1)} %convert_element_type.9.wh_ref, bf16[2,64,576]{2,1,0:T(8,128)(2,1)} %reshape.31.pool_ref, bf16[2,64,576]{2,1,0:T(8,128)(2,1)} %reshape.33.tx_ref, ...), custom_call_target="tpu_custom_call" | custom-call | tf_op jit(solution)/shard_map/pallas_call | solution.py:308
  134.5 0.0 copy-start.7
  134.6 0.6 copy-done.7
  135.2 0.6 slice.3
  135.7 0.0 copy-start.5
  135.7 1.6 %reduce = f32[144]{0:T(256)} reduce(f32[144,1]{1,0:T(8,128)} %get-tuple-element.9, f32[]{:T(128)} %constant.4), dimensions={1}, to_apply=%get-tuple-element.9.reduce_sub_computation | reduce | bytes 1156 | tf_op jit(solution)/shard_map/pallas_call | solution.py:308
  137.3 0.0 copy-done.5
  137.3 0.6 reduce.1
  137.9 2.0 %copy.27 = f32[144,1076]{1,0:T(8,128)} copy(f32[144,1076]{1,0:T(8,128)} %get-tuple-element.16) | data formatting | bytes 1239552
  (1 shorter events, 0.0 us)
Async XLA Ops:
  0.6 3.9 %copy-start.1 = (bf16[64,1152]{1,0:T(8,128)(2,1)S(1)}, bf16[64,1152]{1,0:T(8,128)(2,1)}, u32[]{:S(2)}) copy-start(bf16[64,1152]{1,0:T(8,128)(2,1)} %param.10) | copy-start | bytes 442372
  2.0 1.1 copy-start.4
  3.1 0.7 copy-start.6
  5.1 0.9 copy-start.3
  6.0 1.3 copy-start
  7.3 1.2 copy-start.2
  134.5 0.6 copy-start.7
  135.7 1.6 %copy-start.5 = (f32[1,1076]{1,0:T(1,128)S(1)}, f32[1,1076]{1,0:T(1,128)}, u32[]{:S(2)}) copy-start(f32[1,1076]{1,0:T(1,128)} %get-tuple-element.10) | copy-start | bytes 12916

commit v2 on v1

--- a/solution.py
+++ b/solution.py
@@ -26,9 +26,9 @@
     sizes,
     hs_ref, wh_ref, pool_ref, tx_ref, rm_ref, cm_ref, ls_ref, bias_ref,
     upd_ref, nr_ref, nc_ref, loss_ref,
-    hid, wg, txa, part, proj, img_s, img_r, ug_s, ug_r, mg_s, mga, gz_s, gz,
+    hid, wg, txa, part, pre, summed, proj, img_s, img_r, ug_s, ug_r, mg_s, mga, gp, gz_s, gz,
     rsb, csb, stb,
-    hid_ss, hid_rs, w_ss, w_rs, tz_ss, tp_ss, t_rs, p_ss, p_rs, pair_ss, pair_rs,
+    hid_ss, hid_rs, w_ss, w_rs, tz_ss, tp_ss, t_rs, td_ss, td_rs, pp_ss, pp_rs, p_ss, p_rs, pair_ss, pair_rs,
     mg_ss, mg_rs, g_ss, g_rs, row_ss, row_rs, col_ss, col_rs, st_ss, st_rs,
 ):
     R, C, X, Z, T, Db, Dp, Fb, chunk = sizes
@@ -79,6 +79,33 @@
     def text_place(zs):
         return x * C + zs * L + y
 
+    def neighbours():
+        along_x = [(lax.rem(x + o, X), y) for o in range(1, X)]
+        return along_x + [(x, lax.rem(y + o, L)) for o in range(1, L)]
+
+    def relay(s):
+        for d, direction in enumerate((1, -1)):
+            if s == 0 and d:
+                continue
+            zs = z - direction * s
+            has = jnp.logical_and(zs >= 0, zs < Z)
+            block = jnp.clip(zs, 0, Z - 1)
+            for n, (x2, y2) in enumerate(neighbours()):
+                place = x2 * C + block * L + y2
+                at = txa.at[:, rows(place, T), :]
+                if s:
+                    pl.when(has)(lambda: arrived(at, t_rs.at[place]))
+                else:
+                    arrived(at, t_rs.at[place])
+                h = 0 if n < X - 1 else 1
+                half = txa.at[h, rows(place, T), :]
+                onward = neighbours()[X - 1:] if h == 0 else neighbours()[:X - 1]
+                for m, (x3, y3) in enumerate(onward):
+                    send(
+                        half, half, td_ss.at[d, s, n, m], td_rs.at[place, h],
+                        (x3 * CORES + core, z * L + y3), has if s else None,
+                    )
+
     for s in range(Z):
         for d, direction in enumerate((1, -1)):
             zs = z - direction * s
@@ -92,13 +119,10 @@
                 pl.when(has)(lambda: arrived(at, t_rs.at[place]))
             send(source, at, tz_ss.at[d, s], t_rs.at[place], (r, jnp.clip(nz, 0, Z - 1) * L + y), go)
             if s or d == 0:
-                mine = x * L + y
-                for o in range(1, X * L):
-                    other = lax.rem(mine + o, X * L)
+                for n, (x2, y2) in enumerate(neighbours()):
                     send(
-                        source, at, tp_ss.at[d, s, o], t_rs.at[place],
-                        ((other // L) * CORES + core, z * L + other % L),
-                        has if s else None,
+                        source, at, tp_ss.at[d, s, n], t_rs.at[place],
+                        (x2 * CORES + core, z * L + y2), has if s else None,
                     )
         for d, direction in enumerate((1, -1)):
             zs = z - direction * s
@@ -113,22 +137,41 @@
                 wh_ref if s == 0 else at, at, w_ss.at[d, s], w_rs.at[block],
                 (r, jnp.clip(nz, 0, Z - 1) * L + y), go,
             )
+        if s:
+            relay(s - 1)
     for o in range(1, plane):
         other, _, _ = plane_peer(o)
         arrived(hid.at[rows(other, T)], hid_rs.at[other])
 
     part[...] = dot_nt(hid[...], wg[...])
-    for o in range(1, plane):
-        other, r2, y2 = plane_peer(o)
-        send(part.at[rows(other, T)], proj.at[r, y], p_ss.at[o], p_rs.at[q], (r2, z * L + y2))
-    proj[r, y] = part[rows(q, T)]
-    for o in range(1, plane):
-        other, r2, y2 = plane_peer(o)
-        arrived(proj.at[r2, y2], p_rs.at[other])
+    partner = (x * CORES + (1 - core), c)
+    for o in range(1, X + 1):
+        x2 = lax.rem(x + o, X)
+        send(
+            part.at[rows(x2 * CORES + 1 - core, L * T)], pre.at[x2],
+            pp_ss.at[o], pp_rs.at[x2], partner,
+        )
+    relay(Z - 1)
+    for o in range(1, X + 1):
+        x2 = lax.rem(x + o, X)
+        arrived(pre.at[x2], pp_rs.at[x2])
+        summed[x2] = part[rows(x2 * CORES + core, L * T)] + pre[x2]
+        for k in range(L):
+            y2 = lax.rem(y + 1 + k, L)
+            if o == X and k == L - 1:
+                proj[x, y] = summed[x, rows(y, T)]
+            else:
+                send(
+                    summed.at[x2, rows(y2, T)], proj.at[x, y], p_ss.at[o * L + k],
+                    p_rs.at[x * L + y], (x2 * CORES + core, z * L + y2),
+                )
+    for o in range(1, X * L):
+        other = lax.rem(x * L + y + o, X * L)
+        arrived(proj.at[other // L, other % L], p_rs.at[other])
     mixed = []
     for h in range(L):
         total = proj[0, h]
-        for k in range(1, R):
+        for k in range(1, X):
             total = total + proj[k, h]
         mixed.append(pool_ref[h].astype(F32) + total)
     square = sum(jnp.sum(m * m, axis=1, keepdims=True) for m in mixed)
@@ -136,14 +179,14 @@
     unit = [m / length for m in mixed]
     for h in range(L):
         img_s[h] = unit[h].astype(BF16)
-    partner = (x * CORES + (1 - core), c)
     send(img_s, img_r, pair_ss.at[0], pair_rs.at[0], partner)
 
-    for o in range(1, X * L):
-        other = lax.rem(x * L + y + o, X * L)
-        for zs in range(Z):
-            place = (other // L) * C + zs * L + other % L
-            arrived(txa.at[:, rows(place, T), :], t_rs.at[place])
+    for ox in range(1, X):
+        for oy in range(1, L):
+            for zs in range(Z):
+                place = lax.rem(x + ox, X) * C + zs * L + lax.rem(y + oy, L)
+                for h in range(L):
+                    arrived(txa.at[h, rows(place, T), :], td_rs.at[place, h])
 
     scale = jnp.exp(jnp.full((1, 1), ls_ref[0], F32))
     bias = jnp.full((1, 1), bias_ref[0], F32)
@@ -189,27 +232,63 @@
     inner = sum(jnp.sum(unit[h] * ug[h], axis=1, keepdims=True) for h in range(L))
     for h in range(L):
         mg_s[h] = ((ug[h] - unit[h] * inner) / length).astype(BF16)
-    for o in range(1, plane):
-        _, r2, y2 = plane_peer(o)
-        send(mg_s.at[y2], mga.at[rows(q, T)], mg_ss.at[o], mg_rs.at[q], (r2, z * L + y2))
+    for o in range(1, X * L):
+        other = lax.rem(x * L + y + o, X * L)
+        send(
+            mg_s.at[other % L], mga.at[rows(q, T)], mg_ss.at[o], mg_rs.at[q],
+            ((other // L) * CORES + core, z * L + other % L),
+        )
+    send(mg_s.at[y], mga.at[rows(q, T)], mg_ss.at[0], mg_rs.at[q], partner)
     mga[rows(q, T)] = mg_s[y]
-    for o in range(1, plane):
-        other, _, _ = plane_peer(o)
-        arrived(mga.at[rows(other, T)], mg_rs.at[other])
+    for o in range(1, X * L):
+        other = lax.rem(x * L + y + o, X * L)
+        source = ((other // L) * CORES + core) * L + other % L
+        at = mga.at[rows(source, T)]
+        arrived(at, mg_rs.at[source])
+        send(at, at, mg_ss.at[X * L + o], mg_rs.at[source], partner)
+    for o in range(X * L):
+        other = lax.rem(x * L + y + o, X * L)
+        source = ((other // L) * CORES + 1 - core) * L + other % L
+        arrived(mga.at[rows(source, T)], mg_rs.at[source])
 
     turned = mga[...].T
-    for zs in range(Z):
-        gz_s[zs] = jnp.dot(
-            turned[zs * Dp:(zs + 1) * Dp], hid[...], preferred_element_type=F32
-        ).astype(BF16)
-    for o in range(1, Z):
-        z2 = lax.rem(z + o, Z)
-        send(gz_s.at[z2], gz.at[z], g_ss.at[o], g_rs.at[z], (r, z2 * L + y))
-    upd_ref[...] = own_block(turned, hid, z, Z, Dp, Db)
-    for o in range(1, Z):
-        z2 = lax.rem(z + o, Z)
-        arrived(gz.at[z2], g_rs.at[z2])
-        upd_ref[...] += gz[z2][:Db].astype(F32)
+
+    def own_part(zd):
+        gp[zd] = jnp.dot(turned[zd * Dp:(zd + 1) * Dp], hid[...], preferred_element_type=F32)
+
+    def pass_on(zd, d, direction):
+        first = z == (0 if d == 0 else Z - 1)
+        before = z < zd if d == 0 else z > zd
+
+        def add():
+            arrived(gz.at[d, zd], g_rs.at[d, zd])
+            gz_s[zd] = (gp[zd] + gz[d, zd].astype(F32)).astype(BF16)
+
+        def start():
+            gz_s[zd] = gp[zd].astype(BF16)
+
+        pl.when(jnp.logical_and(before, first))(start)
+        pl.when(jnp.logical_and(before, jnp.logical_not(first)))(add)
+        send(
+            gz_s.at[zd], gz.at[d, zd], g_ss.at[d, zd], g_rs.at[d, zd],
+            (r, jnp.clip(z + direction, 0, Z - 1) * L + y), before,
+        )
+
+    for k in range(Z):
+        up, down = Z - 1 - k, k
+        if k < (Z + 1) // 2:
+            own_part(up)
+            if down != up:
+                own_part(down)
+        pass_on(up, 0, 1)
+        pass_on(down, 1, -1)
+    upd_ref[...] = gp[z][:Db]
+    for d in range(2):
+        def take():
+            arrived(gz.at[d, z], g_rs.at[d, z])
+            upd_ref[...] += gz[d, z][:Db].astype(F32)
+
+        pl.when(z > 0 if d == 0 else z < Z - 1)(take)
     g = upd_ref[...]
 
     sq = g * g + FLOOR_VALUE
@@ -271,13 +350,6 @@
         wait()
 
 
-def own_block(turned, hid, z, Z, Dp, Db):
-    picked = turned[0:Dp]
-    for zs in range(1, Z):
-        picked = jnp.where(z == zs, turned[zs * Dp:(zs + 1) * Dp], picked)
-    return jnp.dot(picked, hid[...], preferred_element_type=F32)[:Db]
-
-
 def per_device(pooled, hidden, text, weight, row_moment, col_moment, log_scale, bias):
     R, C = lax.axis_size("row"), lax.axis_size("col")
     L, X, Z = LOW, R // CORES, C // LOW
@@ -320,20 +392,24 @@
             pltpu.VMEM((F2, Fb), BF16),
             pltpu.VMEM((L, texts, F2), BF16),
             pltpu.VMEM((plane * T, F2), F32),
-            pltpu.VMEM((R, L, T, F2), F32),
+            pltpu.VMEM((X, L * T, F2), F32),
+            pltpu.VMEM((X, L * T, F2), F32),
+            pltpu.VMEM((X, L, T, F2), F32),
             pltpu.VMEM((L, T, F2), BF16),
             pltpu.VMEM((L, T, F2), BF16),
             pltpu.VMEM((L, T, F2), F32),
             pltpu.VMEM((L, T, F2), F32),
             pltpu.VMEM((L, T, F2), BF16),
             pltpu.VMEM((plane * T, F2), BF16),
+            pltpu.VMEM((Z, Dp, Fb), F32),
             pltpu.VMEM((Z, Dp, Fb), BF16),
-            pltpu.VMEM((Z, Dp, Fb), BF16),
+            pltpu.VMEM((2, Z, Dp, Fb), BF16),
             pltpu.VMEM((R, Db, 1), F32),
             pltpu.VMEM((C, 1, Fb), F32),
             pltpu.VMEM((R * C, 1, 128), F32),
-            dma(plane), dma(plane), dma(2, Z), dma(Z), dma(2, Z), dma(2, Z, X * L), dma(X * C),
-            dma(plane), dma(plane), dma(2), dma(2), dma(plane), dma(plane), dma(Z), dma(Z),
+            dma(plane), dma(plane), dma(2, Z), dma(Z), dma(2, Z), dma(2, Z, X + L), dma(X * C),
+            dma(2, Z, X + L, X + L), dma(X * C, L), dma(X + 1), dma(X), dma(X * L + L), dma(X * L),
+            dma(2), dma(2), dma(plane), dma(plane), dma(2, Z), dma(2, Z),
             dma(R), dma(R), dma(C), dma(C), dma(R * C), dma(R * C),
         ],
         compiler_params=pltpu.CompilerParams(

time: 140 us -> 133 us (0.950)
  Pallas kernels: 125 us -> 118 us
    pallas_call x1, Pallas kernels: 125 us -> 118 us  [per_device(): pl.pallas_call(functools.partial(kernel, sizes), out_shape=(jax.ShapeDtyp...]
where the time goes in v2:
time: 133 us
  Pallas kernels  118 us (89%)
  local copies, waits for them, and re-layouts  9 us (7%)
  other arithmetic  4.1 us (3%)
  between operations  2.08 us (2%)
    pallas_call x1, Pallas kernels, per_device(): pl.pallas_call(functools.partial(kernel, sizes), out_shape=(jax.ShapeDtyp...  118 us
    unnamed x17, local copies, waits for them, and re-layouts  3.11 us

profile of v2, /device:TPU:0, one launch (start us, length us, event | category | flops | bytes accessed | tf_op | source)
XLA Modules:
  0.0 132.7 jit_solution(8593903348445643592)
XLA Ops:
  0.6 0.0 copy-start.1
  2.0 0.0 copy-start.4
  2.0 1.0 fusion
  3.0 0.0 copy-done.4
  3.1 0.0 copy-start.6
  3.1 0.6 broadcast_in_dim.14.cm_ref
  3.7 0.1 copy-done.6
  3.7 0.7 copy.17.rm_ref
  4.5 0.0 copy-done.1
  4.5 0.1 fusion.1
  4.6 0.4 reshape.32
  5.0 0.1 copy.22
  5.1 0.0 copy-start.3
  5.1 0.9 reshape.33.tx_ref
  5.9 0.0 copy-done.3
  6.0 0.0 copy-start
  6.0 0.4 reshape.30
  6.3 0.1 copy.23
  6.5 0.9 reshape.31.pool_ref
  7.3 0.0 copy-done
  7.3 0.0 copy-start.2
  7.3 0.8 convert_element_type.9.wh_ref
  8.1 0.4 copy-done.2
  8.5 0.4 reshape.29
  8.9 0.9 copy.21
  9.8 117.5 %shard_map.111 = (f32[144,1076]{1,0:T(8,128)}, f32[144,1]{1,0:T(8,128)}, f32[1,1076]{1,0:T(1,128)}, f32[1,128]{1,0:T(1,128)}) custom-call(bf16[4,64,1076]{2,1,0:T(8,128)(2,1)} %bitcast.15, bf16[144,1076]{1,0:T(8,128)(2,1)} %convert_element_type.9.wh_ref, bf16[2,64,576]{2,1,0:T(8,128)(2,1)} %reshape.31.pool_ref, bf16[2,64,576]{2,1,0:T(8,128)(2,1)} %reshape.33.tx_ref, ...), custom_call_target="tpu_custom_call" | custom-call | tf_op jit(solution)/shard_map/pallas_call | solution.py:380
  127.3 0.0 copy-start.7
  127.4 0.6 copy-done.7
  127.9 0.6 slice.3
  128.5 0.0 copy-start.5
  128.5 1.6 %reduce = f32[144]{0:T(256)} reduce(f32[144,1]{1,0:T(8,128)} %get-tuple-element.9, f32[]{:T(128)} %constant.4), dimensions={1}, to_apply=%get-tuple-element.9.reduce_sub_computation | reduce | bytes 1156 | tf_op jit(solution)/shard_map/pallas_call | solution.py:380
  130.1 0.0 copy-done.5
  130.1 0.6 reduce.1
  130.7 2.0 %copy.27 = f32[144,1076]{1,0:T(8,128)} copy(f32[144,1076]{1,0:T(8,128)} %get-tuple-element.16) | data formatting | bytes 1239552
  (1 shorter events, 0.0 us)
Async XLA Ops:
  0.6 3.9 %copy-start.1 = (bf16[64,1152]{1,0:T(8,128)(2,1)S(1)}, bf16[64,1152]{1,0:T(8,128)(2,1)}, u32[]{:S(2)}) copy-start(bf16[64,1152]{1,0:T(8,128)(2,1)} %param.10) | copy-start | bytes 442372
  2.0 1.1 copy-start.4
  3.1 0.7 copy-start.6
  5.1 0.9 copy-start.3
  6.0 1.3 %copy-start = (f32[144,1076]{1,0:T(8,128)S(1)}, f32[144,1076]{1,0:T(8,128)}, u32[]{:S(2)}) copy-start(f32[144,1076]{1,0:T(8,128)} %param.11) | copy-start | bytes 1859332
  7.3 1.2 copy-start.2
  127.3 0.6 copy-start.7
  128.5 1.6 %copy-start.5 = (f32[1,1076]{1,0:T(1,128)S(1)}, f32[1,1076]{1,0:T(1,128)}, u32[]{:S(2)}) copy-start(f32[1,1076]{1,0:T(1,128)} %get-tuple-element.10) | copy-start | bytes 12916

commit v3 on v2

--- a/solution.py
+++ b/solution.py
@@ -192,20 +192,18 @@
     bias = jnp.full((1, 1), bias_ref[0], F32)
     steps = X * C * T // chunk
 
-    def pairs(images, own):
-        halves = [images[h] for h in range(L)]
+    def pairs():
+        halves = [jnp.concatenate([img_s[h], img_r[h]], axis=0) for h in range(L)]
 
         def step(i, carry):
             loss, grads = carry
             cut = pl.ds(pl.multiple_of(i * chunk, chunk), chunk)
             texts = [txa[h, cut, :] for h in range(L)]
             logits = scale * sum(dot_nt(halves[h], texts[h]) for h in range(L)) + bias
-            if own:
-                row_id = lax.broadcasted_iota(jnp.int32, logits.shape, 0) + own_slot * T
-                col_id = lax.broadcasted_iota(jnp.int32, logits.shape, 1) + i * chunk
-                sign = jnp.where(row_id == col_id, F32(1.0), F32(-1.0))
-            else:
-                sign = F32(-1.0)
+            row_id = lax.broadcasted_iota(jnp.int32, logits.shape, 0)
+            col_id = lax.broadcasted_iota(jnp.int32, logits.shape, 1) + (i * chunk - own_slot * T)
+            match = jnp.logical_and(row_id == col_id, row_id < T)
+            sign = jnp.where(match, F32(1.0), F32(-1.0))
             u = -sign * logits
             e = jnp.exp(-jnp.abs(u))
             loss = loss + jnp.sum(jnp.maximum(u, 0.0) + jnp.log1p(e), axis=1, keepdims=True)
@@ -216,19 +214,20 @@
             )
             return loss, grads
 
-        zero = (jnp.zeros((T, 1), F32), tuple(jnp.zeros((T, Z * Dp), F32) for _ in range(L)))
+        zero = (
+            jnp.zeros((2 * T, 1), F32), tuple(jnp.zeros((2 * T, Z * Dp), F32) for _ in range(L))
+        )
         if steps == 1:
             return step(0, zero)
         return lax.fori_loop(0, steps, step, zero)
 
     arrived(img_r, pair_rs.at[0])
-    loss_b, grads_b = pairs(img_r, False)
+    loss_rows, grads = pairs()
     for h in range(L):
-        ug_s[h] = scale * grads_b[h]
+        ug_s[h] = scale * grads[h][T:]
     send(ug_s, ug_r, pair_ss.at[1], pair_rs.at[1], partner)
-    loss_a, grads_a = pairs(img_s, True)
     arrived(ug_r, pair_rs.at[1])
-    ug = [scale * grads_a[h] + ug_r[h] for h in range(L)]
+    ug = [scale * grads[h][:T] + ug_r[h] for h in range(L)]
     inner = sum(jnp.sum(unit[h] * ug[h], axis=1, keepdims=True) for h in range(L))
     for h in range(L):
         mg_s[h] = ((ug[h] - unit[h] * inner) / length).astype(BF16)
@@ -315,7 +314,7 @@
     raw = g / jnp.sqrt(new_row * new_col)
     upd_ref[...] = raw
     local = jnp.sum(jnp.sum(raw * raw, axis=1, keepdims=True), axis=0, keepdims=True)
-    loss_local = jnp.sum(loss_a + loss_b, axis=0, keepdims=True)
+    loss_local = jnp.sum(loss_rows, axis=0, keepdims=True)
     lane = lax.broadcasted_iota(jnp.int32, (1, 128), 1)
     me = r * C + c
     stb[me] = jnp.where(lane == 0, local, loss_local)

time: 133 us -> 134 us (level)
  no operation moved by 1% of the time
where the time goes in v3:
time: 134 us
  Pallas kernels  119 us (89%)
  local copies, waits for them, and re-layouts  9 us (7%)
  other arithmetic  4.1 us (3%)
  between operations  2.08 us (2%)
    pallas_call x1, Pallas kernels, per_device(): pl.pallas_call(functools.partial(kernel, sizes), out_shape=(jax.ShapeDtyp...  119 us
    unnamed x17, local copies, waits for them, and re-layouts  3.11 us

profile of v3, /device:TPU:0, one launch (start us, length us, event | category | flops | bytes accessed | tf_op | source)
XLA Modules:
  0.0 134.0 jit_solution(15669896444838747577)
XLA Ops:
  0.6 0.0 copy-start.1
  2.0 0.0 copy-start.4
  2.0 1.0 fusion
  3.0 0.0 copy-done.4
  3.1 0.0 copy-start.6
  3.1 0.6 broadcast_in_dim.14.cm_ref
  3.7 0.1 copy-done.6
  3.7 0.7 copy.17.rm_ref
  4.5 0.0 copy-done.1
  4.5 0.1 fusion.1
  4.6 0.4 reshape.32
  5.0 0.1 copy.22
  5.1 0.0 copy-start.3
  5.1 0.9 reshape.33.tx_ref
  5.9 0.0 copy-done.3
  6.0 0.0 copy-start
  6.0 0.4 reshape.30
  6.3 0.1 copy.23
  6.5 0.9 reshape.31.pool_ref
  7.3 0.0 copy-done
  7.3 0.0 copy-start.2
  7.3 0.8 convert_element_type.9.wh_ref
  8.1 0.4 copy-done.2
  8.5 0.4 reshape.29
  8.9 0.9 copy.21
  9.8 118.8 %shard_map.111 = (f32[144,1076]{1,0:T(8,128)}, f32[144,1]{1,0:T(8,128)}, f32[1,1076]{1,0:T(1,128)}, f32[1,128]{1,0:T(1,128)}) custom-call(bf16[4,64,1076]{2,1,0:T(8,128)(2,1)} %bitcast.15, bf16[144,1076]{1,0:T(8,128)(2,1)} %convert_element_type.9.wh_ref, bf16[2,64,576]{2,1,0:T(8,128)(2,1)} %reshape.31.pool_ref, bf16[2,64,576]{2,1,0:T(8,128)(2,1)} %reshape.33.tx_ref, ...), custom_call_target="tpu_custom_call" | custom-call | tf_op jit(solution)/shard_map/pallas_call | solution.py:379
  128.7 0.0 copy-start.7
  128.7 0.6 copy-done.7
  129.3 0.6 slice.3
  129.8 0.0 copy-start.5
  129.8 1.6 %reduce = f32[144]{0:T(256)} reduce(f32[144,1]{1,0:T(8,128)} %get-tuple-element.9, f32[]{:T(128)} %constant.4), dimensions={1}, to_apply=%get-tuple-element.9.reduce_sub_computation | reduce | bytes 1156 | tf_op jit(solution)/shard_map/pallas_call | solution.py:379
  131.4 0.0 copy-done.5
  131.4 0.6 reduce.1
  132.0 2.0 %copy.27 = f32[144,1076]{1,0:T(8,128)} copy(f32[144,1076]{1,0:T(8,128)} %get-tuple-element.16) | data formatting | bytes 1239552
  (1 shorter events, 0.0 us)
Async XLA Ops:
  0.6 3.9 %copy-start.1 = (bf16[64,1152]{1,0:T(8,128)(2,1)S(1)}, bf16[64,1152]{1,0:T(8,128)(2,1)}, u32[]{:S(2)}) copy-start(bf16[64,1152]{1,0:T(8,128)(2,1)} %param.10) | copy-start | bytes 442372
  2.0 1.1 copy-start.4
  3.1 0.7 copy-start.6
  5.1 0.9 copy-start.3
  6.0 1.3 %copy-start = (f32[144,1076]{1,0:T(8,128)S(1)}, f32[144,1076]{1,0:T(8,128)}, u32[]{:S(2)}) copy-start(f32[144,1076]{1,0:T(8,128)} %param.11) | copy-start | bytes 1859332
  7.3 1.2 copy-start.2
  128.7 0.6 copy-start.7
  129.8 1.6 %copy-start.5 = (f32[1,1076]{1,0:T(1,128)S(1)}, f32[1,1076]{1,0:T(1,128)}, u32[]{:S(2)}) copy-start(f32[1,1076]{1,0:T(1,128)} %get-tuple-element.10) | copy-start | bytes 12916
